TPU v7x, 128 devices: a whole 4x4x4 slice. The times are simulated.
128 devices in a mesh: psg: 16 (over x_hi, y, core), qry: 8 (over z, x_lo).
Axes of the slice: x: 4 (x_hi: 2, x_lo: 2; x = x_hi * 2 + x_lo), y: 4, z: 4, core: 2. Of those that a mesh axis runs over, the one named last changes fastest.
Arguments:
- hidden: bfloat16 [1024, 4096], P('qry'), may hold values from -6 to 6
- norm_gain: float32 [4096], replicated, may hold values from 0.5 to 1.5
- proj_weight: bfloat16 [4096, 4096], P('psg', 'qry'), may hold values from -0.09375 to 0.09375
- pq_codes: int32 [32768, 512], P('psg', 'qry'), may hold values from 0 to 255
- codebook: bfloat16 [512, 8, 256], P('qry'), may hold values from -560 to 560
- positives: int32 [1024], replicated, may hold values from 0 to 32767
Outputs:
- losses: float32 [1024], P('qry')
- hidden_grad: bfloat16 [1024, 4096], P('qry')
- weight_grad: float32 [4096, 4096], P('psg', 'qry')
- codebook_grad: float32 [512, 8, 256], P('qry')
All inputs are finite; a program needn't handle non-finite values.
Results may differ from a plain program's by a relative error of at most 0.019.
The roundings to bfloat16 on the way count: a program that leaves them out, or rounds other values in their place, can miss the bound.
Values may be sent and summed in bfloat16 or wider, within the bound.
A program may use at most 128 MiB of HBM per device.

v0:
```python
import jax
import jax.numpy as jnp
from jax import lax
from jax.sharding import Mesh
from jax.sharding import PartitionSpec as P

QRY = ("qry_0", "qry_1")
score_scale = 0.0625
norm_eps = 1e-06


def summed_rows(x, axes, dim):
    if not axes:
        return x
    nearer = lax.psum_scatter(x, axes[0], scatter_dimension=dim, tiled=True)
    return summed_rows(nearer, axes[1:], dim)


def sent_to_all(x, axis):
    copies = jnp.broadcast_to(x, (lax.axis_size(axis), *x.shape))
    return lax.all_to_all(copies, axis, split_axis=0, concat_axis=0, tiled=True)


def gathered_once(x, axis):
    leaves = jax.tree.leaves(x)
    turns = sorted(range(len(leaves)), key=lambda k: -leaves[k].size)
    width = (1, *leaves[turns[0]].shape)[-1]
    lines = [
        jnp.pad(leaves[k].reshape(-1), (0, -leaves[k].size % width)).reshape(-1, width)
        for k in turns
    ]
    both, at, found = (sent_to_all(jnp.concatenate(lines), axis), 0, {})
    for k, line in zip(turns, lines):
        piece = both[:, at : at + len(line)].reshape(len(both), -1)
        found[k] = piece[:, : leaves[k].size].reshape(-1, *leaves[k].shape)
        at += len(line)
    numbers = iter(range(len(leaves)))
    return jax.tree.map(lambda _: found[next(numbers)], x)


def folded_in_pairs(pieces, combine):
    while len(jax.tree.leaves(pieces)[0]) > 1:
        pieces = jax.vmap(combine)(
            *(jax.tree.map(lambda part: part[side::2], pieces) for side in (0, 1))
        )
    return jax.tree.map(lambda part: part[0], pieces)


def joined_all(x, axis, combine):
    pieces = gathered_once(x, axis)
    return folded_in_pairs(pieces, combine)


def code_hot(code_block, book):
    levels = lax.broadcasted_iota(jnp.int32, code_block.shape + (book.shape[2],), 2)
    return (code_block[:, :, None] == levels).astype(jnp.bfloat16)


def per_device(hidden, norm_gain, proj_weight, pq_codes, codebook, positives):
    gathered = lax.all_gather(hidden, QRY, axis=0, tiled=True)
    floats_all = gathered.astype(jnp.float32)
    inverse_all = lax.rsqrt(jnp.mean(floats_all * floats_all, axis=1, keepdims=True) + norm_eps)
    normed = (floats_all * inverse_all * norm_gain[None, :]).astype(jnp.bfloat16)
    columns = proj_weight.shape[1]
    whole_weight = lax.all_gather(proj_weight, "psg", axis=0, tiled=True)
    query_float = jnp.dot(normed, whole_weight, preferred_element_type=jnp.float32)
    queries = query_float.astype(jnp.bfloat16)
    passage_count = pq_codes.shape[0]
    sub_count = codebook.shape[0]
    sub_width = codebook.shape[1]
    block_rows = min(passage_count, 512)
    code_blocks = pq_codes.reshape(passage_count // block_rows, block_rows, sub_count)

    def decode(code_block):
        hot_table = code_hot(code_block, codebook)
        vectors = jnp.einsum(
            "pmk,mdk->pmd", hot_table, codebook, preferred_element_type=jnp.float32
        )
        return vectors.astype(jnp.bfloat16).reshape(block_rows, columns)

    passages = lax.map(decode, code_blocks).reshape(passage_count, columns)
    partial_value = (
        lax.dot_general(
            queries, passages, (((1,), (1,)), ((), ())), preferred_element_type=jnp.float32
        )
        * score_scale
    )
    qry_index = lax.axis_index(QRY)
    own_rows = hidden.shape[0]
    scores = summed_rows(partial_value, QRY, 0)
    row_targets = lax.dynamic_slice_in_dim(positives, qry_index * own_rows, own_rows, 0)
    local_target = row_targets - lax.axis_index("psg") * passage_count
    target = lax.broadcasted_iota(jnp.int32, scores.shape, 1) == local_target[:, None]
    local_max = jnp.max(scores, axis=1)
    positive_part = jnp.sum(jnp.where(target, scores, 0.0), axis=1)
    local_total = jnp.sum(jnp.exp(scores - local_max[:, None]), axis=1)

    def combine(first, second):
        higher = jnp.maximum(first[0], second[0])
        joined = first[1] * jnp.exp(first[0] - higher) + second[1] * jnp.exp(second[0] - higher)
        return (higher, joined, first[2] + second[2])

    row_max, row_total, positive_score = joined_all(
        (local_max, local_total, positive_part), "psg", combine
    )
    losses = jnp.log(row_total) + row_max - positive_score
    score_grad = (
        jnp.exp(scores - row_max[:, None]) / row_total[:, None] - target.astype(jnp.float32)
    ).astype(jnp.bfloat16)
    all_grad = lax.all_gather(score_grad, QRY, axis=0, tiled=True)
    query_part = jnp.dot(all_grad, passages, preferred_element_type=jnp.float32) * score_scale
    query_grad = lax.psum(query_part, "psg").astype(jnp.bfloat16)
    passage_grad = (
        lax.dot_general(
            all_grad, queries, (((0,), (0,)), ((), ())), preferred_element_type=jnp.float32
        )
        * score_scale
    ).astype(jnp.bfloat16)
    grad_blocks = passage_grad.reshape(
        passage_count // block_rows, block_rows, sub_count, sub_width
    )

    def add_book(carry, paired):
        code_block, grad_block = paired
        hot_table = code_hot(code_block, codebook)
        return (
            carry
            + jnp.einsum("pmk,pmd->mdk", hot_table, grad_block, preferred_element_type=jnp.float32),
            None,
        )

    book_part, unused = lax.scan(
        add_book, jnp.zeros(codebook.shape, jnp.float32), (code_blocks, grad_blocks)
    )
    codebook_grad = lax.psum(book_part.astype(jnp.bfloat16), "psg").astype(jnp.float32)
    row_span = proj_weight.shape[0]
    normed_rows = lax.dynamic_slice_in_dim(normed, lax.axis_index("psg") * row_span, row_span, 1)
    weight_grad = lax.dot_general(
        normed_rows, query_grad, (((0,), (0,)), ((), ())), preferred_element_type=jnp.float32
    )
    norm_part = lax.dot_general(
        query_grad, whole_weight, (((1,), (1,)), ((), ())), preferred_element_type=jnp.float32
    )
    norm_back = lax.psum_scatter(
        norm_part.astype(jnp.bfloat16), QRY, scatter_dimension=0, tiled=True
    ).astype(jnp.float32)
    floats_own = hidden.astype(jnp.float32)
    inverse_own = lax.rsqrt(jnp.mean(floats_own * floats_own, axis=1, keepdims=True) + norm_eps)
    scaled = norm_back * norm_gain[None, :]
    hidden_grad = (
        inverse_own * scaled
        - floats_own
        * inverse_own
        * inverse_own
        * inverse_own
        * jnp.mean(scaled * floats_own, axis=1, keepdims=True)
    ).astype(jnp.bfloat16)
    return (losses, hidden_grad, weight_grad, codebook_grad)


def solution(mesh):
    split = Mesh(mesh.devices.reshape(mesh.shape["psg"], 4, 2), ("psg", "qry_0", "qry_1"))
    return jax.shard_map(
        per_device,
        mesh=split,
        in_specs=(P(QRY, None), P(), P("psg", QRY), P("psg", QRY), P(QRY, None, None), P()),
        out_specs=(P(QRY), P(QRY, None), P("psg", QRY), P(QRY, None, None)),
        check_vma=False,
    )
```

profile of v0, /device:TPU:1, one launch (start us, length us, event | category | flops | bytes accessed | tf_op | source)
XLA Modules:
  0.0 852.5 jit_solution(15345686447529952865)
XLA Ops:
  9.8 33.1 %while.21 = (s32[]{:T(128)}, bf16[4,512,512]{2,1,0:T(8,128)(2,1)}, s32[4,512,64]{1,2,0:T(8,128)S(1)}, bf16[64,8,256]{2,1,0:T(8,128)(2,1)}, s32[]{:T(128)}) while((s32[]{:T(128)}, bf16[4,512,512]{2,1,0:T(8,128)(2,1)}, s32[4,512,64]{1,2,0:T(8,128)S(1)}, bf16[64,8,256]{2,1,0:T(8,128)(2,1)}, s32[]{:T(128)}) %tuple.74), condition=%wide.region_2.3_spmd, body=%wide.region_1.2_spmd.sunk | while | flops 142868480 | bytes 3277377 | solution.py:81
  9.8 7.2 fusion.43
  18.1 7.2 fusion.43
  26.4 7.2 fusion.43
  34.6 7.2 fusion.43
  42.9 138.0 %all-gather.4.cloned.1.call-done = bf16[1024,4096]{1,0:T(8,128)(2,1)} async-done(((bf16[128,4096]{1,0:T(8,128)(2,1)}), bf16[1024,4096]{1,0:T(8,128)(2,1)}) %all-gather.4.cloned.1.call-update) | async-done | bytes 8388624 | tf_op jit(solution)/shard_map/all_gather | solution.py:60
  186.0 10.3 %fusion.12 = bf16[1024,4096]{1,0:T(8,128)(2,1)} fusion(bf16[1024,4096]{1,0:T(8,128)(2,1)} %all-gather.4.cloned.1.call-done, f32[4096]{0:T(1024)S(1)} %copy-done.1, f32[1024]{0:T(1024)S(1)} %add_rsqrt_fusion), kind=kLoop, calls=%fused_computation.19 | loop fusion | flops 16777216 | bytes 16797696 | tf_op jit(solution)/shard_map/convert_element_type | solution.py:63
  196.3 43.5 %all-gather.6.cloned.1.call-done = bf16[4096,512]{1,0:T(8,128)(2,1)} async-done(((bf16[256,512]{1,0:T(8,128)(2,1)}), bf16[4096,512]{1,0:T(8,128)(2,1)}) %all-gather.6.cloned.1.call-update) | async-done | bytes 4194320 | tf_op jit(solution)/shard_map/all_gather | solution.py:65
  239.8 9.1 %convolution_convert_fusion.1 = bf16[1024,512]{1,0:T(8,128)(2,1)S(1)} fusion(bf16[1024,4096]{1,0:T(8,128)(2,1)} %fusion.12, bf16[4096,512]{1,0:T(8,128)(2,1)} %all-gather.6.cloned.1.call-done), kind=kOutput, calls=%fused_computation.35 | convolution fusion | flops 4295491584 | bytes 13631488 | tf_op jit(solution)/shard_map/dot_general | solution.py:66
  255.5 78.3 %reduce-scatter.4.cloned.1.call-done = f32[256,2048]{1,0:T(8,128)} async-done(((f32[1024,2048]{1,0:T(8,128)}), f32[256,2048]{1,0:T(8,128)}) %reduce-scatter.4.cloned.1.call-update) | async-done | bytes 2097168 | tf_op jit(solution)/shard_map/reduce_scatter | solution.py:15
  334.6 35.3 %reduce-scatter.6.cloned.1.call-done = f32[128,2048]{1,0:T(8,128)} async-done(((f32[256,2048]{1,0:T(8,128)}), f32[128,2048]{1,0:T(8,128)}) %reduce-scatter.6.cloned.1.call-update) | async-done | bytes 1048592 | tf_op jit(solution)/shard_map/reduce_scatter | solution.py:15
  372.9 14.4 %all_to_all.5 = f32[16,3,128]{2,1,0:T(4,128)S(1)} all-to-all(f32[16,3,128]{2,1,0:T(4,128)S(1)} %broadcast_in_dim.28), channel_id=1, replica_groups=mesh['psg'=16,'qry_0'=4,'qry_1'=2] {'psg'}, dimensions={0} | all-to-all | bytes 49152 | tf_op jit(solution)/shard_map/all_to_all | solution.py:21
  390.8 87.4 %all-gather.8.cloned.1.call-done = bf16[1024,2048]{1,0:T(8,128)(2,1)} async-done(((bf16[128,2048]{1,0:T(8,128)(2,1)}), bf16[1024,2048]{1,0:T(8,128)(2,1)}) %all-gather.8.cloned.1.call-update) | async-done | bytes 4194320 | tf_op jit(solution)/shard_map/all_gather | solution.py:110
  478.2 5.9 multiply_convert_fusion
  493.1 35.0 %while.22 = (s32[]{:T(128)}, f32[64,8,256]{2,1,0:T(8,128)S(1)}, bf16[4,512,64,8]{1,3,2,0:T(8,128)(2,1)}, s32[4,512,64]{1,2,0:T(8,128)S(1)}, s32[]{:T(128)}, /*index=5*/s32[]{:T(128)}) while((s32[]{:T(128)}, f32[64,8,256]{2,1,0:T(8,128)S(1)}, bf16[4,512,64,8]{1,3,2,0:T(8,128)(2,1)}, s32[4,512,64]{1,2,0:T(8,128)S(1)}, s32[]{:T(128)}, ...), condition=%wide.region_13.14_spmd.clone, body=%wide.region_12.13_spmd.clone.sunk | while | flops 142868480 | bytes 1966675 | solution.py:132
  493.1 8.7 %fusion.45 = f32[64,8,256]{2,1,0:T(8,128)S(1)} fusion(s32[512,64]{0,1:T(8,128)S(1)} %dynamic-slice_bitcast_fusion.5, f32[64,8,256]{2,1,0:T(8,128)S(1)} %get-tuple-element.191, bf16[4,512,64,8]{1,3,2,0:T(8,128)(2,1)} %get-tuple-element.198, s32[]{:T(128)} %get-tuple-element.190, pred[]{:T(512)S(6)} %compare.3), kind=kOutput, calls=%fused_computation.10.clone.1 | convolution fusion | flops 142868480 | bytes 1704449 | tf_op jit(solution)/shard_map/while/body/eval_jaxpr/pmk,pmd->mdk/dot_general | solution.py:128
  501.9 8.7 %fusion.45 = f32[64,8,256]{2,1,0:T(8,128)S(1)} fusion(s32[512,64]{0,1:T(8,128)S(1)} %dynamic-slice_bitcast_fusion.5, f32[64,8,256]{2,1,0:T(8,128)S(1)} %get-tuple-element.191, bf16[4,512,64,8]{1,3,2,0:T(8,128)(2,1)} %get-tuple-element.198, s32[]{:T(128)} %get-tuple-element.190, pred[]{:T(512)S(6)} %compare.3), kind=kOutput, calls=%fused_computation.10.clone.1 | convolution fusion | flops 142868480 | bytes 1704449 | tf_op jit(solution)/shard_map/while/body/eval_jaxpr/pmk,pmd->mdk/dot_general | solution.py:128
  510.6 8.7 %fusion.45 = f32[64,8,256]{2,1,0:T(8,128)S(1)} fusion(s32[512,64]{0,1:T(8,128)S(1)} %dynamic-slice_bitcast_fusion.5, f32[64,8,256]{2,1,0:T(8,128)S(1)} %get-tuple-element.191, bf16[4,512,64,8]{1,3,2,0:T(8,128)(2,1)} %get-tuple-element.198, s32[]{:T(128)} %get-tuple-element.190, pred[]{:T(512)S(6)} %compare.3), kind=kOutput, calls=%fused_computation.10.clone.1 | convolution fusion | flops 142868480 | bytes 1704449 | tf_op jit(solution)/shard_map/while/body/eval_jaxpr/pmk,pmd->mdk/dot_general | solution.py:128
  519.4 8.7 %fusion.45 = f32[64,8,256]{2,1,0:T(8,128)S(1)} fusion(s32[512,64]{0,1:T(8,128)S(1)} %dynamic-slice_bitcast_fusion.5, f32[64,8,256]{2,1,0:T(8,128)S(1)} %get-tuple-element.191, bf16[4,512,64,8]{1,3,2,0:T(8,128)(2,1)} %get-tuple-element.198, s32[]{:T(128)} %get-tuple-element.190, pred[]{:T(512)S(6)} %compare.3), kind=kOutput, calls=%fused_computation.10.clone.1 | convolution fusion | flops 142868480 | bytes 1704449 | tf_op jit(solution)/shard_map/while/body/eval_jaxpr/pmk,pmd->mdk/dot_general | solution.py:128
  528.9 6.5 convolution_multiply_fusion.1
  535.4 77.4 %all-reduce.4 = bf16[1024,512]{1,0:T(8,128)(2,1)S(1)} all-reduce(f32[1024,512]{1,0:T(8,128)} %convolution_multiply_fusion.1), channel_id=1, replica_groups=mesh['psg'=16,'qry_0'=4,'qry_1'=2] {'psg'}, use_global_device_ids=true, to_apply=%region_9.10 | all-reduce | flops 524288 | bytes 3145728 | tf_op jit(solution)/shard_map/psum | solution.py:112
  612.8 8.9 %convolution_convert_fusion = bf16[1024,4096]{1,0:T(8,128)(2,1)} fusion(bf16[4096,512]{1,0:T(8,128)(2,1)} %all-gather.6.cloned.1.call-done, bf16[1024,512]{1,0:T(8,128)(2,1)S(1)} %all-reduce.4), kind=kOutput, calls=%fused_computation.20 | convolution fusion | flops 4299161600 | bytes 13631488 | tf_op jit(solution)/shard_map/dot_general | solution.py:141
  624.2 44.1 %all-reduce.3.cloned.1.call-done = bf16[64,8,256]{2,1,0:T(8,128)(2,1)} async-done(((bf16[64,8,256]{2,1,0:T(8,128)(2,1)}), bf16[64,8,256]{2,1,0:T(8,128)(2,1)}) %all-reduce.3.cloned.1.call-update) | async-done | bytes 262160 | tf_op jit(solution)/shard_map/psum | solution.py:135
  670.0 170.9 %reduce-scatter.8.cloned.1.call-done = bf16[128,4096]{1,0:T(8,128)(2,1)} async-done(((bf16[1024,4096]{1,0:T(8,128)(2,1)}), bf16[128,4096]{1,0:T(8,128)(2,1)}) %reduce-scatter.8.cloned.1.call-update) | async-done | bytes 1048592 | tf_op jit(solution)/shard_map/reduce_scatter | solution.py:144
  (87 shorter events, 44.6 us)
Async XLA Ops:
  7.2 173.7 %all-gather.4.cloned.1.call-start = ((), (), s32[]{:S(2)}) async-start(), calls=%async_computation.4 | async-start | bytes 9437184 | tf_op jit(solution)/shard_map/all_gather | solution.py:60
  7.9 231.9 %all-gather.6.cloned.1.call-start = ((), (), s32[]{:S(2)}) async-start(), calls=%async_computation.5 | async-start | bytes 4456448 | tf_op jit(solution)/shard_map/all_gather | solution.py:65
  8.6 325.1 %reduce-scatter.4.cloned.1.call-start = ((), (), s32[]{:S(2)}) async-start(), calls=%async_computation.6 | async-start | bytes 10485760 | tf_op jit(solution)/shard_map/reduce_scatter | solution.py:15
  42.9 143.1 %copy-start.1 = (f32[4096]{0:T(1024)S(1)}, f32[4096]{0:T(1024)}, u32[]{:S(2)}) copy-start(f32[4096]{0:T(1024)} %param.11) | copy-start | bytes 49156
  196.3 53.5 %copy-start.2 = (bf16[4,512,512]{2,1,0:T(8,128)(2,1)S(1)}, bf16[4,512,512]{2,1,0:T(8,128)(2,1)}, u32[]{:S(2)}) copy-start(bf16[4,512,512]{2,1,0:T(8,128)(2,1)} %get-tuple-element.48) | copy-start | bytes 6291460
  248.9 1.0 copy-start.3
  255.5 222.7 %copy-start.4 = (bf16[1024,512]{1,0:T(8,128)(2,1)S(1)}, bf16[1024,512]{1,0:T(8,128)(2,1)}, u32[]{:S(2)}) copy-start(bf16[1024,512]{1,0:T(8,128)(2,1)} %copy-done.3) | copy-start | bytes 3145732
  255.5 114.4 %reduce-scatter.6.cloned.1.call-start = ((), (), s32[]{:S(2)}) async-start(), calls=%async_computation.7 | async-start | bytes 3145728 | tf_op jit(solution)/shard_map/reduce_scatter | solution.py:15
  333.8 144.4 %all-gather.8.cloned.1.call-start = ((), (), s32[]{:S(2)}) async-start(), calls=%async_computation.8 | async-start | bytes 4718592 | tf_op jit(solution)/shard_map/all_gather | solution.py:110
  390.7 277.5 %all-reduce.3.cloned.1.call-start = ((), (), s32[]{:S(2)}) async-start(), calls=%async_computation.10 | async-start | bytes 524288 | tf_op jit(solution)/shard_map/psum | solution.py:135
  528.9 312.1 %reduce-scatter.8.cloned.1.call-start = ((), (), s32[]{:S(2)}) async-start(), calls=%async_computation.9 | async-start | bytes 9437184 | tf_op jit(solution)/shard_map/reduce_scatter | solution.py:144
  621.8 219.2 %copy-start = (bf16[128,4096]{1,0:T(8,128)(2,1)S(1)}, bf16[128,4096]{1,0:T(8,128)(2,1)}, u32[]{:S(2)}) copy-start(bf16[128,4096]{1,0:T(8,128)(2,1)} %param.10) | copy-start | bytes 3145732
Sparse Core Ops, SparseCore 0:
  9.6 171.2 all-gather.3
  183.4 56.3 all-gather.5
  255.6 78.1 reduce-scatter.3
  336.0 33.8 reduce-scatter.5
  390.9 87.2 all-gather.7
  529.0 139.1 all-reduce.2
  670.6 170.2 reduce-scatter.7
where the time goes:
time: 854 us; the launch traced here: 852 us
  waiting for transfers between devices  599 us (70%)
  matrix products  102 us (12%)
  blocking collectives  91.8 us (11%)
  other arithmetic  29.4 us (3%)
  local copies, waits for them, and re-layouts  15.8 us (2%)
  between operations  14.3 us (2%)
    reduce_scatter x1, waiting for transfers between devices, per_device(): lax.psum_scatter(norm_part.astype(jnp.bfloat16), QRY, scatter_dimension=0...  171 us
    all_gather x1, waiting for transfers between devices, per_device(): gathered = lax.all_gather(hidden, QRY, axis=0, tiled=True)  138 us
    reduce_scatter x2, waiting for transfers between devices, summed_rows(): nearer = lax.psum_scatter(x, axes[0], scatter_dimension=dim, tiled=True)  114 us
    all_gather x1, waiting for transfers between devices, per_device(): all_grad = lax.all_gather(score_grad, QRY, axis=0, tiled=True)  87.4 us
    psum x1, blocking collectives, per_device(): query_grad = lax.psum(query_part, 'psg').astype(jnp.bfloat16)  77.4 us
    psum x1, waiting for transfers between devices, per_device(): lax.psum(book_part.astype(jnp.bfloat16), 'psg').astype(jnp.float32)  44.1 us
    all_gather x1, waiting for transfers between devices, per_device(): whole_weight = lax.all_gather(proj_weight, 'psg', axis=0, tiled=True)  43.5 us
    dot_general x4, matrix products, add_book(): jnp.einsum('pmk,pmd->mdk', hot_table, grad_block, preferred_element_type=...  34.9 us
  transfers between devices with their start and end apart: 7, of which 7 were waited for; matrix products, arithmetic and copies ran while one was open for 8% of the time, Pallas kernels for 0%

commit v1 on v0

--- a/solution.py
+++ b/solution.py
@@ -109,7 +109,7 @@
     ).astype(jnp.bfloat16)
     all_grad = lax.all_gather(score_grad, QRY, axis=0, tiled=True)
     query_part = jnp.dot(all_grad, passages, preferred_element_type=jnp.float32) * score_scale
-    query_grad = lax.psum(query_part, "psg").astype(jnp.bfloat16)
+    query_grad = jnp.sum(lax.all_gather(query_part, axis_name="psg"), 0).astype(jnp.bfloat16)
     passage_grad = (
         lax.dot_general(
             all_grad, queries, (((0,), (0,)), ((), ())), preferred_element_type=jnp.float32

time: 854 us -> 995 us (1.17)
  waiting for transfers between devices: 599 us -> 797 us
  blocking collectives: 91.8 us -> 14.4 us
  other arithmetic: 29.4 us -> 42.2 us
    all_gather x0 -> x1, waiting for transfers between devices: none -> 127 us  [per_device(): lax.all_gather(query_part, axis_name='psg')]
    psum x1 -> x0, blocking collectives: 77.4 us -> none  [per_device(): query_grad = lax.psum(query_part, 'psg').astype(jnp.bfloat16)]
    psum x1, waiting for transfers between devices: 44.1 us -> 117 us  [per_device(): lax.psum(book_part.astype(jnp.bfloat16), 'psg').astype(jnp.float32)]
    reduce_sum x0 -> x1, other arithmetic: none -> 12.8 us  [per_device(): jnp.sum(lax.all_gather(query_part, axis_name='psg'), 0).astype(jnp.bfloat16)]
  transfers between devices with their start and end apart: 7 -> 8, of which waited for: 7 -> 8; matrix products, arithmetic and copies ran while one was open for 8% -> 14% of each run, Pallas kernels for 0% -> 0%
where the time goes in v1:
time: 995 us; the launch traced here: 994 us
  waiting for transfers between devices  797 us (80%)
  matrix products  111 us (11%)
  other arithmetic  42.2 us (4%)
  local copies, waits for them, and re-layouts  14.7 us (1%)
  blocking collectives  14.4 us (1%)
  between operations  14.3 us (1%)
    reduce_scatter x1, waiting for transfers between devices, per_device(): lax.psum_scatter(norm_part.astype(jnp.bfloat16), QRY, scatter_dimension=0...  169 us
    all_gather x1, waiting for transfers between devices, per_device(): gathered = lax.all_gather(hidden, QRY, axis=0, tiled=True)  138 us
    all_gather x1, waiting for transfers between devices, per_device(): lax.all_gather(query_part, axis_name='psg')  127 us
    psum x1, waiting for transfers between devices, per_device(): lax.psum(book_part.astype(jnp.bfloat16), 'psg').astype(jnp.float32)  117 us
    reduce_scatter x2, waiting for transfers between devices, summed_rows(): nearer = lax.psum_scatter(x, axes[0], scatter_dimension=dim, tiled=True)  114 us
    all_gather x1, waiting for transfers between devices, per_device(): all_grad = lax.all_gather(score_grad, QRY, axis=0, tiled=True)  87.4 us
    dot_general x4, matrix products, add_book(): jnp.einsum('pmk,pmd->mdk', hot_table, grad_block, preferred_element_type=...  44 us
    all_gather x1, waiting for transfers between devices, per_device(): whole_weight = lax.all_gather(proj_weight, 'psg', axis=0, tiled=True)  43.4 us
  transfers between devices with their start and end apart: 8, of which 8 were waited for; matrix products, arithmetic and copies ran while one was open for 14% of the time, Pallas kernels for 0%

profile of v1, /device:TPU:1, one launch (start us, length us, event | category | flops | bytes accessed | tf_op | source)
XLA Modules:
  0.0 993.5 jit_solution(10880669878259769187)
XLA Ops:
  9.8 33.1 %while.21 = (s32[]{:T(128)}, bf16[4,512,512]{2,1,0:T(8,128)(2,1)}, s32[4,512,64]{1,2,0:T(8,128)S(1)}, bf16[64,8,256]{2,1,0:T(8,128)(2,1)}, s32[]{:T(128)}) while((s32[]{:T(128)}, bf16[4,512,512]{2,1,0:T(8,128)(2,1)}, s32[4,512,64]{1,2,0:T(8,128)S(1)}, bf16[64,8,256]{2,1,0:T(8,128)(2,1)}, s32[]{:T(128)}) %tuple.76), condition=%wide.region_2.3_spmd, body=%wide.region_1.2_spmd.sunk | while | flops 142868480 | bytes 3276877 | solution.py:81
  9.8 7.2 fusion.43
  18.1 7.2 fusion.43
  26.4 7.2 fusion.43
  34.7 7.2 fusion.43
  42.9 138.1 %all-gather.6.cloned.1.call-done = bf16[1024,4096]{1,0:T(8,128)(2,1)} async-done(((bf16[128,4096]{1,0:T(8,128)(2,1)}), bf16[1024,4096]{1,0:T(8,128)(2,1)}) %all-gather.6.cloned.1.call-update) | async-done | bytes 8388624 | tf_op jit(solution)/shard_map/all_gather | solution.py:60
  186.1 10.3 %fusion.12 = bf16[1024,4096]{1,0:T(8,128)(2,1)} fusion(bf16[1024,4096]{1,0:T(8,128)(2,1)} %all-gather.6.cloned.1.call-done, f32[4096]{0:T(1024)S(1)} %copy-done.1, f32[1024]{0:T(1024)S(1)} %add_rsqrt_fusion), kind=kLoop, calls=%fused_computation.19 | loop fusion | flops 16777216 | bytes 16797696 | tf_op jit(solution)/shard_map/convert_element_type | solution.py:63
  196.4 43.4 %all-gather.8.cloned.1.call-done = bf16[4096,512]{1,0:T(8,128)(2,1)} async-done(((bf16[256,512]{1,0:T(8,128)(2,1)}), bf16[4096,512]{1,0:T(8,128)(2,1)}) %all-gather.8.cloned.1.call-update) | async-done | bytes 4194320 | tf_op jit(solution)/shard_map/all_gather | solution.py:65
  239.8 9.0 convolution_convert_fusion.1
  255.5 78.3 %reduce-scatter.4.cloned.1.call-done = f32[256,2048]{1,0:T(8,128)} async-done(((f32[1024,2048]{1,0:T(8,128)}), f32[256,2048]{1,0:T(8,128)}) %reduce-scatter.4.cloned.1.call-update) | async-done | bytes 2097168 | tf_op jit(solution)/shard_map/reduce_scatter | solution.py:15
  334.6 35.3 %reduce-scatter.6.cloned.1.call-done = f32[128,2048]{1,0:T(8,128)} async-done(((f32[256,2048]{1,0:T(8,128)}), f32[128,2048]{1,0:T(8,128)}) %reduce-scatter.6.cloned.1.call-update) | async-done | bytes 1048592 | tf_op jit(solution)/shard_map/reduce_scatter | solution.py:15
  372.9 14.4 %all_to_all.5 = f32[16,3,128]{2,1,0:T(4,128)S(1)} all-to-all(f32[16,3,128]{2,1,0:T(4,128)S(1)} %broadcast_in_dim.28), channel_id=1, replica_groups=mesh['psg'=16,'qry_0'=4,'qry_1'=2] {'psg'}, dimensions={0} | all-to-all | bytes 49152 | tf_op jit(solution)/shard_map/all_to_all | solution.py:21
  390.8 87.4 %all-gather.10.cloned.1.call-done = bf16[1024,2048]{1,0:T(8,128)(2,1)} async-done(((bf16[128,2048]{1,0:T(8,128)(2,1)}), bf16[1024,2048]{1,0:T(8,128)(2,1)}) %all-gather.10.cloned.1.call-update) | async-done | bytes 4194320 | tf_op jit(solution)/shard_map/all_gather | solution.py:110
  484.1 6.2 multiply_convert_fusion
  498.3 44.1 %while.22 = (s32[]{:T(128)}, f32[64,8,256]{2,1,0:T(8,128)S(1)}, bf16[4,512,64,8]{1,3,2,0:T(8,128)(2,1)S(1)}, s32[4,512,64]{1,2,0:T(8,128)S(1)}, s32[]{:T(128)}, /*index=5*/s32[]{:T(128)}) while((s32[]{:T(128)}, f32[64,8,256]{2,1,0:T(8,128)S(1)}, bf16[4,512,64,8]{1,3,2,0:T(8,128)(2,1)S(1)}, s32[4,512,64]{1,2,0:T(8,128)S(1)}, ...), condition=%wide.region_13.14_spmd.clone, body=%wide.region_12.13_spmd.clone.sunk | while | flops 142868480 | bytes 1966175 | solution.py:132
  498.3 11.0 %fusion.45 = f32[64,8,256]{2,1,0:T(8,128)S(1)} fusion(s32[512,64]{0,1:T(8,128)S(1)} %dynamic-slice_bitcast_fusion.5, f32[64,8,256]{2,1,0:T(8,128)S(1)} %get-tuple-element.191, bf16[4,512,64,8]{1,3,2,0:T(8,128)(2,1)S(1)} %get-tuple-element.198, s32[]{:T(128)S(6)} %copy.39, pred[]{:T(512)S(6)} %compare.3), kind=kOutput, calls=%fused_computation.10.clone.1 | convolution fusion | flops 142868480 | bytes 1703941 | tf_op jit(solution)/shard_map/while/body/eval_jaxpr/pmk,pmd->mdk/dot_general | solution.py:128
  509.3 11.0 %fusion.45 = f32[64,8,256]{2,1,0:T(8,128)S(1)} fusion(s32[512,64]{0,1:T(8,128)S(1)} %dynamic-slice_bitcast_fusion.5, f32[64,8,256]{2,1,0:T(8,128)S(1)} %get-tuple-element.191, bf16[4,512,64,8]{1,3,2,0:T(8,128)(2,1)S(1)} %get-tuple-element.198, s32[]{:T(128)S(6)} %copy.39, pred[]{:T(512)S(6)} %compare.3), kind=kOutput, calls=%fused_computation.10.clone.1 | convolution fusion | flops 142868480 | bytes 1703941 | tf_op jit(solution)/shard_map/while/body/eval_jaxpr/pmk,pmd->mdk/dot_general | solution.py:128
  520.3 11.0 %fusion.45 = f32[64,8,256]{2,1,0:T(8,128)S(1)} fusion(s32[512,64]{0,1:T(8,128)S(1)} %dynamic-slice_bitcast_fusion.5, f32[64,8,256]{2,1,0:T(8,128)S(1)} %get-tuple-element.191, bf16[4,512,64,8]{1,3,2,0:T(8,128)(2,1)S(1)} %get-tuple-element.198, s32[]{:T(128)S(6)} %copy.39, pred[]{:T(512)S(6)} %compare.3), kind=kOutput, calls=%fused_computation.10.clone.1 | convolution fusion | flops 142868480 | bytes 1703941 | tf_op jit(solution)/shard_map/while/body/eval_jaxpr/pmk,pmd->mdk/dot_general | solution.py:128
  531.4 11.0 %fusion.45 = f32[64,8,256]{2,1,0:T(8,128)S(1)} fusion(s32[512,64]{0,1:T(8,128)S(1)} %dynamic-slice_bitcast_fusion.5, f32[64,8,256]{2,1,0:T(8,128)S(1)} %get-tuple-element.191, bf16[4,512,64,8]{1,3,2,0:T(8,128)(2,1)S(1)} %get-tuple-element.198, s32[]{:T(128)S(6)} %copy.39, pred[]{:T(512)S(6)} %compare.3), kind=kOutput, calls=%fused_computation.10.clone.1 | convolution fusion | flops 142868480 | bytes 1703941 | tf_op jit(solution)/shard_map/while/body/eval_jaxpr/pmk,pmd->mdk/dot_general | solution.py:128
  543.2 127.0 %all-gather.12.cloned.1.call-done = f32[16384,512]{1,0:T(8,128)} async-done(((f32[1024,512]{1,0:T(8,128)}), f32[16384,512]{1,0:T(8,128)}) %all-gather.12.cloned.1.call-update) | async-done | bytes 33554448 | tf_op jit(solution)/shard_map/all_gather | solution.py:112
  670.2 12.8 %reduce_sum.58 = bf16[1024,512]{1,0:T(8,128)(2,1)S(1)} reduce(f32[16,1024,512]{2,1,0:T(8,128)} %bitcast.57, f32[]{:T(128)} %constant.17.clone.1), dimensions={0}, to_apply=%region_9.10 | reduce | flops 7864320 | bytes 34603012 | tf_op jit(solution)/shard_map/reduce_sum | solution.py:112
  683.0 9.0 convolution_convert_fusion
  692.0 117.2 %all-reduce.2.cloned.1.call-done = bf16[64,8,256]{2,1,0:T(8,128)(2,1)} async-done(((bf16[64,8,256]{2,1,0:T(8,128)(2,1)}), bf16[64,8,256]{2,1,0:T(8,128)(2,1)}) %all-reduce.2.cloned.1.call-update) | async-done | bytes 262160 | tf_op jit(solution)/shard_map/psum | solution.py:135
  813.3 168.6 %reduce-scatter.8.cloned.1.call-done = bf16[128,4096]{1,0:T(8,128)(2,1)} async-done(((bf16[1024,4096]{1,0:T(8,128)(2,1)}), bf16[128,4096]{1,0:T(8,128)(2,1)}) %reduce-scatter.8.cloned.1.call-update) | async-done | bytes 1048592 | tf_op jit(solution)/shard_map/reduce_scatter | solution.py:144
  (88 shorter events, 49.3 us)
Async XLA Ops:
  7.2 173.8 %all-gather.6.cloned.1.call-start = ((), (), s32[]{:S(2)}) async-start(), calls=%async_computation.4 | async-start | bytes 9437184 | tf_op jit(solution)/shard_map/all_gather | solution.py:60
  7.9 231.9 %all-gather.8.cloned.1.call-start = ((), (), s32[]{:S(2)}) async-start(), calls=%async_computation.5 | async-start | bytes 4456448 | tf_op jit(solution)/shard_map/all_gather | solution.py:65
  8.6 325.1 %reduce-scatter.4.cloned.1.call-start = ((), (), s32[]{:S(2)}) async-start(), calls=%async_computation.6 | async-start | bytes 10485760 | tf_op jit(solution)/shard_map/reduce_scatter | solution.py:15
  42.9 143.2 %copy-start.1 = (f32[4096]{0:T(1024)S(1)}, f32[4096]{0:T(1024)}, u32[]{:S(2)}) copy-start(f32[4096]{0:T(1024)} %param.11) | copy-start | bytes 49156
  196.4 53.4 %copy-start.2 = (bf16[4,512,512]{2,1,0:T(8,128)(2,1)S(1)}, bf16[4,512,512]{2,1,0:T(8,128)(2,1)}, u32[]{:S(2)}) copy-start(bf16[4,512,512]{2,1,0:T(8,128)(2,1)} %get-tuple-element.48) | copy-start | bytes 6291460
  248.8 1.0 copy-start.3
  255.4 114.4 %reduce-scatter.6.cloned.1.call-start = ((), (), s32[]{:S(2)}) async-start(), calls=%async_computation.7 | async-start | bytes 3145728 | tf_op jit(solution)/shard_map/reduce_scatter | solution.py:15
  333.8 144.3 %all-gather.10.cloned.1.call-start = ((), (), s32[]{:S(2)}) async-start(), calls=%async_computation.8 | async-start | bytes 4718592 | tf_op jit(solution)/shard_map/all_gather | solution.py:110
  390.7 279.5 %all-gather.12.cloned.1.call-start = ((), (), s32[]{:S(2)}) async-start(), calls=%async_computation.11 | async-start | bytes 35651584 | tf_op jit(solution)/shard_map/all_gather | solution.py:112
  484.0 325.2 %all-reduce.2.cloned.1.call-start = ((), (), s32[]{:S(2)}) async-start(), calls=%async_computation.10 | async-start | bytes 524288 | tf_op jit(solution)/shard_map/psum | solution.py:135
  543.1 438.8 %reduce-scatter.8.cloned.1.call-start = ((), (), s32[]{:S(2)}) async-start(), calls=%async_computation.9 | async-start | bytes 9437184 | tf_op jit(solution)/shard_map/reduce_scatter | solution.py:144
  692.0 290.0 %copy-start = (bf16[128,4096]{1,0:T(8,128)(2,1)S(1)}, bf16[128,4096]{1,0:T(8,128)(2,1)}, u32[]{:S(2)}) copy-start(bf16[128,4096]{1,0:T(8,128)(2,1)} %param.10) | copy-start | bytes 3145732
Sparse Core Ops, SparseCore 0:
  9.6 171.3 all-gather.5
  183.5 56.2 all-gather.7
  255.6 78.1 reduce-scatter.3
  336.0 33.8 reduce-scatter.5
  390.8 87.2 all-gather.9
  484.1 186.0 all-gather.11
  673.2 135.9 all-reduce.1
  811.6 170.2 reduce-scatter.7
